TPU v7x, 512 devices: a whole 4x8x8 slice. The times are simulated.
512 devices in a mesh: batch: 32 (over z, x), head: 16 (over y, core).
Axes of the slice: x: 4, y: 8, z: 8, core: 2. Of those that a mesh axis runs over, the one named last changes fastest.
Arguments:
- tokens: bfloat16 [16384, 2048], P('batch', 'head'), may hold values from -96 to 96
- lengths: int32 [128], P('batch'), may hold values from 1 to 128
- states: float32 [128, 16, 128, 128], P('batch', 'head'), may hold values from -3 to 3
- norm_gain: float32 [2048], replicated, may hold values from 0.1 to 1.9
- mix_weight: bfloat16 [2048, 14336], P(None, 'head'), may hold values from -0.125 to 0.125
- rate_weight: bfloat16 [2048, 64], P(None, 'head'), may hold values from -0.5524272 to 0.5524272
- decay_rate: float32 [16], P('head'), may hold values from 0.0005 to 0.03
- head_gain: float32 [128], replicated, may hold values from 0.1 to 1.9
- out_weight: bfloat16 [2048, 2048], P('head'), may hold values from -0.125 to 0.125
- final_gain: float32 [2048], replicated, may hold values from 0.1 to 1.9
- vocab_table: bfloat16 [16384, 2048], P(('batch', 'head')), may hold values from -50.8233 to 50.8233
- next_token: int32 [128], replicated, may hold values from 0 to 16383
Outputs:
- mixed: bfloat16 [16384, 2048], P('batch', 'head')
- new_state: float32 [128, 16, 128, 128], P('batch', 'head')
- log_likelihood: float32 [128], replicated
All inputs are finite; a program needn't handle non-finite values.
Results may differ from a plain program's by a relative error of at most 0.0058.
The roundings to bfloat16 on the way count: a program that leaves them out, or rounds other values in their place, can miss the bound.
Values may be sent and summed in bfloat16 or wider, within the bound.
A program may use at most 64 MiB of HBM per device.

v0:
```python
import jax
import jax.numpy as jnp
from jax import lax
from jax.sharding import Mesh
from jax.sharding import PartitionSpec as P

HEAD_DIM = 128
REFLECT = 3
NEW_POSITIONS = 128
HEAD = ("head_0", "head_1")
BATCH_HEAD = ("batch_0", "batch_1", "head_0", "head_1")
BATCH = ("batch_0", "batch_1")
ROW_EPSILON = 1e-05
KEY_EPSILON = 1e-06
HIGHEST_PRECISION = lax.Precision.HIGHEST


def all_in_one(array, axis):
    leaves = jax.tree.leaves(array)
    order = sorted(range(len(leaves)), key=lambda k: -leaves[k].size)
    width = (1, *leaves[order[0]].shape)[-1]
    lines = [
        jnp.pad(leaves[k].reshape(-1), (0, -leaves[k].size % width)).reshape(-1, width)
        for k in order
    ]
    both, at, found = (lax.all_gather(jnp.concatenate(lines), axis), 0, {})
    for k, line in zip(order, lines):
        share = both[:, at : at + len(line)].reshape(len(both), -1)
        found[k] = share[:, : leaves[k].size].reshape(-1, *leaves[k].shape)
        at += len(line)
    numbers = iter(range(len(leaves)))
    return jax.tree.map(lambda _: found[next(numbers)], array)


def joined_all(array, axes, combine):
    for axis in axes:
        pieces = all_in_one(array, axis)
        array = jax.tree.map(lambda part: part[0], pieces)
        for k in range(1, lax.axis_size(axis)):
            array = combine(array, jax.tree.map(lambda part: part[k], pieces))
    return array


def delta_block(queries, key_rows, value_rows, beta_rows, log_decay, start_state):
    positions = key_rows.shape[0]
    reflections = key_rows.shape[1]
    total_steps = positions * reflections
    flat_keys = key_rows.reshape(total_steps, key_rows.shape[2])
    flat_values = value_rows.reshape(total_steps, value_rows.shape[2])
    flat_betas = beta_rows.reshape(total_steps)
    padding = jnp.zeros((positions, reflections - 1), log_decay.dtype)
    step_decay = jnp.concatenate([log_decay[:, None], padding], axis=1).reshape(total_steps)
    cumulative = jnp.cumsum(step_decay)
    step_index = jnp.arange(total_steps)
    earlier = step_index[:, None] > step_index[None, :]
    decay_ratio = jnp.exp(jnp.where(earlier, cumulative[:, None] - cumulative[None, :], -jnp.inf))
    key_gram = jnp.dot(flat_keys, flat_keys.T, precision=HIGHEST_PRECISION)
    system = (
        jnp.eye(total_steps, dtype=key_gram.dtype) + flat_betas[:, None] * decay_ratio * key_gram
    )
    start_image = jnp.dot(flat_keys, start_state.T, precision=HIGHEST_PRECISION)
    source = flat_betas[:, None] * (flat_values - jnp.exp(cumulative)[:, None] * start_image)
    updates = jax.scipy.linalg.solve_triangular(system, source, lower=True, unit_diagonal=True)
    query_cumulative = cumulative.reshape(positions, reflections)[:, reflections - 1]
    query_step = step_index.reshape(positions, reflections)[:, reflections - 1]
    visible = step_index[None, :] <= query_step[:, None]
    weights = jnp.exp(jnp.where(visible, query_cumulative[:, None] - cumulative[None, :], -jnp.inf))
    scores = jnp.dot(queries, flat_keys.T, precision=HIGHEST_PRECISION) * weights
    attended = jnp.exp(query_cumulative)[:, None] * jnp.dot(
        queries, start_state.T, precision=HIGHEST_PRECISION
    )
    attended = attended + jnp.dot(scores, updates, precision=HIGHEST_PRECISION)
    tail_decay = jnp.exp(cumulative[total_steps - 1] - cumulative)
    new_state = jnp.exp(cumulative[total_steps - 1]) * start_state
    new_state = new_state + jnp.dot(
        updates.T, tail_decay[:, None] * flat_keys, precision=HIGHEST_PRECISION
    )
    return (attended, new_state)


def head_inputs(projected, rate_logits, valid_mask, decay_rate):
    queries = jax.nn.silu(projected[:, :, :, 0])
    key_rows = jax.nn.silu(projected[:, :, :, 1 : REFLECT + 1])
    key_rows = key_rows * lax.rsqrt(
        jnp.sum(key_rows * key_rows, axis=-1, keepdims=True) + KEY_EPSILON
    )
    value_rows = jax.nn.silu(projected[:, :, :, REFLECT + 1 :])
    beta_rows = jnp.where(
        valid_mask[:, :, None, None], 2.0 * jax.nn.sigmoid(rate_logits[..., :REFLECT]), 0.0
    )
    log_decay = jnp.where(
        valid_mask[:, :, None], -decay_rate * jax.nn.softplus(rate_logits[..., REFLECT]), 0.0
    )
    return (queries, key_rows, value_rows, beta_rows, log_decay)


def run_heads(queries, key_rows, value_rows, beta_rows, log_decay, start_states):
    per_head = jax.vmap(delta_block, in_axes=(1, 1, 1, 1, 1, 0), out_axes=(1, 0))
    per_sequence = jax.vmap(per_head)
    return per_sequence(queries, key_rows, value_rows, beta_rows, log_decay, start_states)


def head_norm(attended, head_gain):
    factor = lax.rsqrt(jnp.mean(attended * attended, axis=-1, keepdims=True) + ROW_EPSILON)
    return (attended * factor * head_gain).astype(jnp.bfloat16)


def combine_totals(earlier_part, later_part):
    highest = jnp.maximum(earlier_part[0], later_part[0])
    summed = earlier_part[1] * jnp.exp(earlier_part[0] - highest) + later_part[1] * jnp.exp(
        later_part[0] - highest
    )
    return (highest, summed, earlier_part[2] + later_part[2])


def on_device(
    tokens,
    lengths,
    states,
    norm_gain,
    mix_weight,
    rate_weight,
    decay_rate,
    head_gain,
    out_weight,
    final_gain,
    vocab_table,
    next_token,
):
    sequences = lengths.shape[0]
    local_rows = tokens.shape[0]
    local_width = tokens.shape[1]
    model_width = norm_gain.shape[0]
    local_heads = states.shape[1]
    wide_portion = lax.all_gather(tokens, HEAD, axis=1, tiled=True).astype(jnp.float32)
    scaled = (wide_portion * norm_gain).astype(jnp.bfloat16)
    projected = jnp.dot(scaled, mix_weight, preferred_element_type=jnp.float32)
    rate_logits = jnp.dot(scaled, rate_weight, preferred_element_type=jnp.float32)
    squares = jnp.sum(wide_portion * wide_portion, axis=1)
    projected, rate_logits, squares = (projected, rate_logits, squares)
    inverse = lax.rsqrt(squares / model_width + ROW_EPSILON)
    projected = (projected * inverse[:, None]).reshape(
        sequences, NEW_POSITIONS, local_heads, 2 * REFLECT + 1, HEAD_DIM
    )
    rate_logits = (rate_logits * inverse[:, None]).reshape(
        sequences, NEW_POSITIONS, local_heads, REFLECT + 1
    )
    valid_mask = jnp.arange(NEW_POSITIONS)[None, :] < lengths[:, None]
    queries, key_rows, value_rows, beta_rows, log_decay = head_inputs(
        projected, rate_logits, valid_mask, decay_rate
    )
    attended, new_state = run_heads(queries, key_rows, value_rows, beta_rows, log_decay, states)
    normed = head_norm(attended, head_gain).reshape(local_rows, local_heads * HEAD_DIM)
    columns = lax.all_to_all(out_weight, HEAD, split_axis=1, concat_axis=0, tiled=True)
    mix_sum = jnp.dot(
        lax.all_gather(normed, HEAD, axis=1, tiled=True),
        columns,
        preferred_element_type=jnp.float32,
    )
    mixed = (tokens.astype(jnp.float32) + mix_sum).astype(jnp.bfloat16)
    last_index = (lengths - 1)[:, None, None]
    last_rows = jnp.take_along_axis(
        mixed.reshape(sequences, NEW_POSITIONS, local_width), last_index, axis=1
    )[:, 0]
    gathered = lax.all_gather(last_rows[None], BATCH_HEAD, axis=0, tiled=True)
    batch_count = lax.axis_size(BATCH)
    head_count = lax.axis_size(HEAD)
    everyone = gathered.reshape(batch_count, head_count, sequences, local_width).transpose(
        0, 2, 1, 3
    )
    everyone = everyone.reshape(batch_count * sequences, model_width)
    widened_all = everyone.astype(jnp.float32)
    factor = lax.rsqrt(jnp.mean(widened_all * widened_all, axis=1, keepdims=True) + ROW_EPSILON)
    hidden = (widened_all * factor * final_gain).astype(jnp.bfloat16)
    logits = jnp.dot(hidden, vocab_table.T, preferred_element_type=jnp.float32)
    vocab_here = vocab_table.shape[0]
    vocab_ids = lax.axis_index(BATCH_HEAD) * vocab_here + jnp.arange(vocab_here)
    largest = jnp.max(logits, axis=1)
    exp_total = jnp.sum(jnp.exp(logits - largest[:, None]), axis=1)
    target = jnp.sum(jnp.where(vocab_ids[None, :] == next_token[:, None], logits, 0.0), axis=1)
    largest, exp_total, target = joined_all(
        (largest, exp_total, target), BATCH_HEAD, combine_totals
    )
    return (mixed, new_state, target - (largest + jnp.log(exp_total)))


def solution(mesh):
    torus = Mesh(mesh.devices.reshape(8, 4, 8, 2), ("batch_0", "batch_1", "head_0", "head_1"))
    placed = (
        P(BATCH, HEAD),
        P(BATCH),
        P(BATCH, HEAD, None, None),
        P(),
        P(None, HEAD),
        P(None, HEAD),
        P(HEAD),
        P(),
        P(HEAD, None),
        P(),
        P(BATCH_HEAD, None),
        P(),
    )
    return jax.shard_map(
        on_device,
        mesh=torus,
        in_specs=placed,
        out_specs=(P(BATCH, HEAD), P(BATCH, HEAD, None, None), P()),
        check_vma=False,
    )
```

profile of v0, /device:TPU:1, one launch (start us, length us, event | category | flops | bytes accessed | tf_op | source)
XLA Modules:
  0.0 411.4 jit_solution(3345442622129094462)
XLA Ops:
  7.2 0.7 all-gather.11.cloned.1.call-update
  8.6 0.6 iota_multiply_fusion
  9.2 1.1 fusion.28
  10.4 1.2 iota_compare_fusion.5
  11.6 0.7 iota_compare_fusion.4
  12.3 0.9 iota_compare_fusion.1
  13.2 45.9 %all-gather.11.cloned.1.call-done = bf16[512,2048]{1,0:T(8,128)(2,1)} async-done(((bf16[512,128]{1,0:T(8,128)(2,1)}), bf16[512,2048]{1,0:T(8,128)(2,1)}) %all-gather.11.cloned.1.call-update) | async-done | bytes 2097168 | tf_op jit(solution)/shard_map/all_gather | solution.py:135
  59.1 2.1 fusion.1
  61.2 2.4 fusion.19
  63.9 0.2 reshape.1829
  64.1 1.2 reduce-window.6
  65.3 0.7 slice.491
  66.0 0.2 reshape.1830
  66.2 5.6 %fusion.6 = f32[512,896]{1,0:T(8,128)} fusion(bf16[2048,896]{1,0:T(8,128)(2,1)} %param.16, bf16[512,2048]{1,0:T(8,128)(2,1)S(1)} %copy-done.1, f32[2048]{0:T(1024)S(1)} %copy-done.21, f32[512]{0:T(512)S(1)} %add_rsqrt_fusion.2), kind=kOutput, calls=%fused_computation.10 | convolution fusion | flops 1882652672 | bytes 7612416 | tf_op jit(solution)/shard_map/dot_general | solution.py:137
  71.8 1.6 reshape.1914
  73.4 0.9 slice.495
  74.3 1.4 fusion.132
  75.7 0.8 copy.214
  76.7 0.2 reshape.1833
  76.9 1.7 divide_multiply_fusion
  78.6 0.3 broadcast_multiply_fusion.1
  78.9 0.5 copy.221
  79.8 0.2 mul.576
  80.0 0.5 copy.229
  80.5 0.2 fusion.42
  80.8 0.4 copy-done.14
  81.3 5.3 %select_add_fusion = f32[4,384,384]{2,1,0:T(8,128)} fusion(f32[384,384]{1,0:T(8,128)} %get-tuple-element.100, f32[4,384]{1,0:T(4,128)S(1)} %get-tuple-element.86, f32[4,384]{1,0:T(4,128)S(1)} %mul.576, f32[384,384]{1,0:T(8,128)} %get-tuple-element.99, pred[384,384]{1,0:T(8,128)(4,1)S(1)} %copy-done.7, pred[384,384]{1,0:T(8,128)(4,1)S(1)} %copy-done.8, ...), kind=kOutput, calls=%fused_computation.7 | convolution fusion | flops 910098432 | bytes 4632576 | tf_op jit(solution)/shard_map/vmap(vmap())/dot_general | solution.py:57
  86.6 11.4 %while.1 = (s32[]{:T(128)}, f32[4,1,384,384]{3,2,1,0:T(8,128)}, s32[3,2]{0,1:T(2,128)S(1)}, f32[3,4,1,128,128]{4,3,0,2,1:T(8,128)}, s32[]{:T(128)}) while((s32[]{:T(128)}, f32[4,1,384,384]{3,2,1,0:T(8,128)}, s32[3,2]{0,1:T(2,128)S(1)}, f32[3,4,1,128,128]{4,3,0,2,1:T(8,128)}, s32[]{:T(128)}) %tuple.58), condition=%wide.while_cond, body=%wide.while_body.sunk | while | flops 2 | bytes 525421 | solution.py:63
  86.7 0.6 fusion.144
  87.2 3.2 bitcast_dynamic-update-slice_fusion.2
  90.5 0.6 fusion.144
  91.0 3.2 bitcast_dynamic-update-slice_fusion.2
  94.3 0.6 fusion.144
  94.9 3.1 bitcast_dynamic-update-slice_fusion.2
  98.0 118.9 %custom-call.4 = f32[4,1,3,128,128]{3,4,2,1,0:T(8,128)S(1)} custom-call(f32[4,1,3,128,128]{4,3,2,1,0:T(8,128)} %bitcast.624), custom_call_target="InvertDiagBlocksLowerTriangular" | custom-call | tf_op jit(solution)/shard_map/vmap(vmap(jit(_solve_triangular)))/triangular_solve | solution.py:63
  216.9 0.9 fusion.11
  217.8 0.6 fusion.34
  218.4 1.4 fusion.13
  219.8 0.6 convolution_bitcast_fusion.2
  220.4 1.7 fusion.15
  222.1 0.6 convolution_bitcast_fusion
  222.7 0.4 fusion.39
  223.1 0.7 convolution_multiply_fusion.2
  223.9 1.1 convolution_multiply_fusion.1
  224.9 1.0 multiply_reduce_fusion.2
  225.9 0.8 fusion.36
  226.8 1.0 copy.235
  227.8 5.1 %all-to-all-start = ((bf16[128,16,128]{0,2,1:T(8,128)(2,1)}), bf16[128,16,128]{0,2,1:T(8,128)(2,1)S(1)}, u32[]{:S(2)}, u32[]{:S(2)}) async-start(bf16[128,16,128]{0,2,1:T(8,128)(2,1)} %bitcast.33), calls=%async_computation | async-start | bytes 1048576 | tf_op jit(solution)/shard_map/all_to_all | solution.py:154
  233.0 18.5 %all-to-all-done = bf16[128,16,128]{0,2,1:T(8,128)(2,1)S(1)} async-done(((bf16[128,16,128]{0,2,1:T(8,128)(2,1)}), bf16[128,16,128]{0,2,1:T(8,128)(2,1)S(1)}, u32[]{:S(2)}, u32[]{:S(2)}) %all-to-all-start) | async-done | bytes 524320 | tf_op jit(solution)/shard_map/all_to_all | solution.py:154
  251.5 0.3 copy.236
  251.8 0.7 exp.430
  252.6 0.5 broadcast_multiply_fusion
  253.1 2.1 fusion.17
  255.3 18.9 %all-gather.13.cloned.1.call-done = bf16[512,2048]{1,0:T(8,128)(2,1)} async-done(((bf16[512,128]{1,0:T(8,128)(2,1)}), bf16[512,2048]{1,0:T(8,128)(2,1)}) %all-gather.13.cloned.1.call-update) | async-done | bytes 2097168 | tf_op jit(solution)/shard_map/all_gather | solution.py:156
  274.2 2.3 fusion.18
  276.5 0.6 gather_fusion
  277.2 70.2 %all_gather.35 = bf16[512,4,128]{2,1,0:T(4,128)(2,1)S(1)} all-gather(bf16[1,4,128]{2,1,0:T(4,128)(2,1)S(1)} %bitcast_select_fusion), channel_id=1, replica_groups=mesh['batch_0'=8,'batch_1'=4,'head_0'=8,'head_1'=2] {'batch_0','batch_1'..., dimensions={0}, use_global_device_ids=true | all-gather | bytes 525312 | tf_op jit(solution)/shard_map/all_gather | solution.py:165
  347.4 0.6 multiply_reduce_fusion
  348.3 0.5 fusion.133
  348.9 15.8 %all-gather.4 = f32[8,3,128]{2,1,0:T(4,128)S(1)} all-gather(f32[1,3,128]{2,1,0:T(4,128)S(1)} %maximum_bitcast_fusion.5), channel_id=2, replica_groups=mesh['batch_0'=8,'batch_1'=4,'head_0'=8,'head_1'=2] {'batch_0'}, dimensions={0}, use_global_device_ids=true | all-gather | bytes 13824 | tf_op jit(solution)/shard_map/all_gather | solution.py:26
  364.8 8.1 %all-gather.5 = f32[4,3,128]{2,1,0:T(4,128)S(1)} all-gather(f32[1,3,128]{2,1,0:T(4,128)S(1)} %maximum_bitcast_fusion.6), channel_id=3, replica_groups=mesh['batch_0'=8,'batch_1'=4,'head_0'=8,'head_1'=2] {'batch_1'}, dimensions={0}, use_global_device_ids=true | all-gather | bytes 7680 | tf_op jit(solution)/shard_map/all_gather | solution.py:26
  373.0 15.6 %all-gather.6 = f32[8,3,128]{2,1,0:T(4,128)S(1)} all-gather(f32[1,3,128]{2,1,0:T(4,128)S(1)} %maximum_bitcast_fusion.7), channel_id=4, replica_groups=mesh['batch_0'=8,'batch_1'=4,'head_0'=8,'head_1'=2] {'head_0'}, dimensions={0}, use_global_device_ids=true | all-gather | bytes 13824 | tf_op jit(solution)/shard_map/all_gather | solution.py:26
  388.6 15.4 %all-gather.7 = f32[2,3,128]{2,1,0:T(4,128)S(1)} all-gather(f32[1,3,128]{2,1,0:T(4,128)S(1)} %maximum_bitcast_fusion.8), channel_id=5, replica_groups=mesh['batch_0'=8,'batch_1'=4,'head_0'=8,'head_1'=2] {'head_1'}, dimensions={0}, use_global_device_ids=true | all-gather | bytes 4608 | tf_op jit(solution)/shard_map/all_gather | solution.py:26
  404.0 0.5 fusion.49
  (99 shorter events, 2.1 us)
Async XLA Ops:
  7.2 341.1 %copy-start = (bf16[32,2048]{1,0:T(8,128)(2,1)S(1)}, bf16[32,2048]{1,0:T(8,128)(2,1)}, u32[]{:S(2)}) copy-start(bf16[32,2048]{1,0:T(8,128)(2,1)} %param.22) | copy-start | bytes 393220
  7.2 54.0 %copy-start.20 = (bf16[2048,4]{0,1:T(4,128)(2,1)S(1)}, bf16[2048,4]{0,1:T(4,128)(2,1)}, u32[]{:S(2)}) copy-start(bf16[2048,4]{0,1:T(4,128)(2,1)} %param.17) | copy-start | bytes 49156
  7.2 54.0 %copy-start.21 = (f32[2048]{0:T(1024)S(1)}, f32[2048]{0:T(1024)}, u32[]{:S(2)}) copy-start(f32[2048]{0:T(1024)} %param.15) | copy-start | bytes 24580
  7.2 51.9 %all-gather.11.cloned.1.call-start = ((), (), s32[]{:S(2)}) async-start(), calls=%async_computation.1 | async-start | bytes 2228224 | tf_op jit(solution)/shard_map/all_gather | solution.py:135
  7.9 266.2 %all-gather.13.cloned.1.call-start = ((), (), s32[]{:S(2)}) async-start(), calls=%async_computation.2 | async-start | bytes 2228224 | tf_op jit(solution)/shard_map/all_gather | solution.py:156
  13.2 50.4 %copy-start.17 = (s32[4]{0:T(128)S(1)}, s32[4]{0:T(128)}, u32[]{:S(2)}) copy-start(s32[4]{0:T(128)} %param.13) | copy-start | bytes 52
  61.2 5.0 %copy-start.1 = (bf16[512,2048]{1,0:T(8,128)(2,1)S(1)}, bf16[512,2048]{1,0:T(8,128)(2,1)}, u32[]{:S(2)}) copy-start(bf16[512,2048]{1,0:T(8,128)(2,1)} %all-gather.11.cloned.1.call-done) | copy-start | bytes 6291460
  63.6 13.0 %copy-start.10 = (f32[4,128,1,4]{1,0,3,2:T(4,128)}, f32[4,128,1,4]{1,0,3,2:T(4,128)S(1)}, u32[]{:S(2)}) copy-start(f32[4,128,1,4]{1,0,3,2:T(4,128)S(1)} %reshape.1828) | copy-start | bytes 24580
  78.6 0.9 slice-start
  78.6 1.1 copy-start.16
  78.9 2.4 copy-start.7
  78.9 2.3 copy-start.8
  80.7 0.5 copy-start.14
  81.2 5.3 %copy-start.11 = (f32[4,384]{1,0:T(4,128)}, f32[4,384]{1,0:T(4,128)S(1)}, u32[]{:S(2)}) copy-start(f32[4,384]{1,0:T(4,128)S(1)} %get-tuple-element.86) | copy-start | bytes 18436
  81.3 5.3 %copy-start.22 = (s32[3]{0:T(128)S(1)}, s32[3]{0:T(128)}, u32[]{:S(2)}) copy-start(s32[3]{0:T(128)} %iota_multiply_fusion) | copy-start | bytes 40
  86.6 130.3 %copy-start.2 = (f32[4,1,128,128]{3,2,1,0:T(8,128)S(1)}, f32[4,1,128,128]{3,2,1,0:T(8,128)}, u32[]{:S(2)}) copy-start(f32[4,1,128,128]{3,2,1,0:T(8,128)} %param.14) | copy-start | bytes 786436
  218.4 4.7 %copy-start.5 = (f32[4,128,1,1,128]{4,3,1,0,2:T(1,128)S(1)}, f32[4,128,1,1,128]{4,3,1,0,2:T(1,128)}, u32[]{:S(2)}) copy-start(f32[4,128,1,1,128]{4,3,1,0,2:T(1,128)} %slice.495) | copy-start | bytes 786436
  219.8 4.0 copy-start.9
  219.8 4.0 copy-start.12
  223.8 2.1 copy-start.15
  223.8 2.9 copy-start.4
  225.9 7.0 %copy-start.18 = (s32[4]{0:T(128)S(1)}, s32[4]{0:T(128)}, u32[]{:S(2)}) copy-start(s32[4]{0:T(128)} %param.13) | copy-start | bytes 52
  227.8 23.8 %all-to-all-start = ((bf16[128,16,128]{0,2,1:T(8,128)(2,1)}), bf16[128,16,128]{0,2,1:T(8,128)(2,1)S(1)}, u32[]{:S(2)}, u32[]{:S(2)}) async-start(bf16[128,16,128]{0,2,1:T(8,128)(2,1)} %bitcast.33), calls=%async_computation | async-start | bytes 1048576 | tf_op jit(solution)/shard_map/all_to_all | solution.py:154
  251.5 22.6 %copy-start.3 = (bf16[512,128]{1,0:T(8,128)(2,1)S(1)}, bf16[512,128]{1,0:T(8,128)(2,1)}, u32[]{:S(2)}) copy-start(bf16[512,128]{1,0:T(8,128)(2,1)} %param.12) | copy-start | bytes 393220
  274.2 74.1 %copy-start.13 = (f32[2048]{0:T(1024)S(1)}, f32[2048]{0:T(1024)}, u32[]{:S(2)}) copy-start(f32[2048]{0:T(1024)} %param.21) | copy-start | bytes 24580
  276.5 128.1 %copy-start.6 = (bf16[512,128]{1,0:T(8,128)(2,1)}, bf16[512,128]{1,0:T(8,128)(2,1)S(1)}, u32[]{:S(2)}) copy-start(bf16[512,128]{1,0:T(8,128)(2,1)S(1)} %fusion.18) | copy-start | bytes 393220
  276.5 72.3 %copy-start.19 = (s32[128]{0:T(128)S(1)}, s32[128]{0:T(128)}, u32[]{:S(2)}) copy-start(s32[128]{0:T(128)} %param.23) | copy-start | bytes 1540
Sparse Core Ops, SparseCore 0:
  10.1 48.9 all-gather.10
  226.9 47.2 all-gather.12
where the time goes:
time: 412 us; the launch traced here: 411 us
  other arithmetic  132 us (32%)
  blocking collectives  125 us (30%)
  waiting for transfers between devices  84 us (20%)
  matrix products  26.7 us (6%)
  local copies, waits for them, and re-layouts  22.6 us (5%)
  between operations  15.3 us (4%)
  starting transfers between devices  5.22 us (1%)
    another operation x3, other arithmetic, delta_block(): jax.scipy.linalg.solve_triangular(system, source, lower=True, unit_diagon...  119 us
    all_gather x1, blocking collectives, on_device(): gathered = lax.all_gather(last_rows[None], BATCH_HEAD, axis=0, tiled=True)  70.2 us
    all_gather x4, blocking collectives, all_in_one(): both, at, found = (lax.all_gather(jnp.concatenate(lines), axis), 0, {})  55 us
    all_gather x1, waiting for transfers between devices, on_device(): lax.all_gather(tokens, HEAD, axis=1, tiled=True).astype(jnp.float32)  45.9 us
    all_gather x1, waiting for transfers between devices, on_device(): lax.all_gather(normed, HEAD, axis=1, tiled=True)  18.9 us
    all_to_all x1, waiting for transfers between devices, on_device(): lax.all_to_all(out_weight, HEAD, split_axis=1, concat_axis=0, tiled=True)  18.5 us
    another operation x20, local copies, waits for them, and re-layouts  13.7 us
  transfers between devices with their start and end apart: 3, of which 3 were waited for; matrix products, arithmetic and copies ran while one was open for 2% of the time, Pallas kernels for 0%

commit v1 on v0

--- a/solution.py
+++ b/solution.py
@@ -162,7 +162,10 @@
     last_rows = jnp.take_along_axis(
         mixed.reshape(sequences, NEW_POSITIONS, local_width), last_index, axis=1
     )[:, 0]
-    gathered = lax.all_gather(last_rows[None], BATCH_HEAD, axis=0, tiled=True)
+    gathered = jnp.concatenate(
+        lax.all_to_all(jnp.stack([last_rows[None]] * lax.axis_size(BATCH_HEAD)), BATCH_HEAD, 0, 0),
+        axis=0,
+    )
     batch_count = lax.axis_size(BATCH)
     head_count = lax.axis_size(HEAD)
     everyone = gathered.reshape(batch_count, head_count, sequences, local_width).transpose(

time: 412 us -> 380 us (0.922)
  blocking collectives: 125 us -> 54 us
  waiting for transfers between devices: 84 us -> 106 us
  starting transfers between devices: 5.22 us -> 20.7 us
    all_gather x1 -> x0, blocking collectives: 70.2 us -> none  [on_device(): gathered = lax.all_gather(last_rows[None], BATCH_HEAD, axis=0, tiled=True)]
    all_to_all x0 -> x1, waiting for transfers between devices: none -> 19.9 us  [on_device(): lax.all_to_all(jnp.stack([last_rows[None]] * lax.axis_size(BATCH_HEAD)),...]
    all_to_all x0 -> x1, starting transfers between devices: none -> 15.5 us  [on_device(): lax.all_to_all(jnp.stack([last_rows[None]] * lax.axis_size(BATCH_HEAD)),...]
    another operation x20 -> x21, local copies, waits for them, and re-layouts: 13.7 us -> 14.5 us
  transfers between devices with their start and end apart: 3 -> 4, of which waited for: 3 -> 4; matrix products, arithmetic and copies ran while one was open for 2% -> 3% of each run, Pallas kernels for 0% -> 0%
where the time goes in v1:
time: 380 us; the launch traced here: 379 us
  other arithmetic  132 us (35%)
  waiting for transfers between devices  106 us (28%)
  blocking collectives  54 us (14%)
  matrix products  26.7 us (7%)
  local copies, waits for them, and re-layouts  24 us (6%)
  starting transfers between devices  20.7 us (5%)
  between operations  15.3 us (4%)
    another operation x3, other arithmetic, delta_block(): jax.scipy.linalg.solve_triangular(system, source, lower=True, unit_diagon...  119 us
    all_gather x4, blocking collectives, all_in_one(): both, at, found = (lax.all_gather(jnp.concatenate(lines), axis), 0, {})  54 us
    all_gather x1, waiting for transfers between devices, on_device(): lax.all_gather(tokens, HEAD, axis=1, tiled=True).astype(jnp.float32)  45.8 us
    all_gather x1, waiting for transfers between devices, on_device(): lax.all_gather(normed, HEAD, axis=1, tiled=True)  20.5 us
    all_to_all x1, waiting for transfers between devices, on_device(): lax.all_to_all(jnp.stack([last_rows[None]] * lax.axis_size(BATCH_HEAD)),...  19.9 us
    all_to_all x1, waiting for transfers between devices, on_device(): lax.all_to_all(out_weight, HEAD, split_axis=1, concat_axis=0, tiled=True)  19 us
    all_to_all x1, starting transfers between devices, on_device(): lax.all_to_all(jnp.stack([last_rows[None]] * lax.axis_size(BATCH_HEAD)),...  15.5 us
    another operation x20, local copies, waits for them, and re-layouts  13.6 us
  transfers between devices with their start and end apart: 4, of which 4 were waited for; matrix products, arithmetic and copies ran while one was open for 3% of the time, Pallas kernels for 0%

profile of v1, /device:TPU:1, one launch (start us, length us, event | category | flops | bytes accessed | tf_op | source)
XLA Modules:
  0.0 378.9 jit_solution(9148590202398283064)
XLA Ops:
  7.2 0.7 all-gather.11.cloned.1.call-update
  8.6 0.6 iota_multiply_fusion
  9.2 1.1 fusion.28
  10.4 1.3 iota_compare_fusion.5
  11.7 0.7 iota_compare_fusion.4
  12.4 0.9 iota_compare_fusion.1
  13.2 45.8 %all-gather.11.cloned.1.call-done = bf16[512,2048]{1,0:T(8,128)(2,1)} async-done(((bf16[512,128]{1,0:T(8,128)(2,1)}), bf16[512,2048]{1,0:T(8,128)(2,1)}) %all-gather.11.cloned.1.call-update) | async-done | bytes 2097168 | tf_op jit(solution)/shard_map/all_gather | solution.py:135
  59.1 2.1 fusion.1
  61.2 2.4 fusion.19
  63.9 0.2 reshape.1820
  64.1 1.2 reduce-window.6
  65.3 0.7 slice.491
  66.0 0.2 reshape.1821
  66.2 5.6 %fusion.6 = f32[512,896]{1,0:T(8,128)} fusion(bf16[2048,896]{1,0:T(8,128)(2,1)} %param.16, bf16[512,2048]{1,0:T(8,128)(2,1)S(1)} %copy-done.1, f32[2048]{0:T(1024)S(1)} %copy-done.21, f32[512]{0:T(512)S(1)} %add_rsqrt_fusion.2), kind=kOutput, calls=%fused_computation.10 | convolution fusion | flops 1882652672 | bytes 7612416 | tf_op jit(solution)/shard_map/dot_general | solution.py:137
  71.8 1.6 reshape.1905
  73.4 0.9 slice.495
  74.3 1.4 fusion.132
  75.8 0.8 copy.181
  76.8 0.2 reshape.1824
  77.0 1.7 divide_multiply_fusion
  78.7 0.3 broadcast_multiply_fusion.1
  79.0 0.5 copy.188
  79.9 0.2 mul.576
  80.1 0.5 copy.196
  80.9 0.4 copy-done.13
  81.3 5.3 %select_add_fusion = f32[4,384,384]{2,1,0:T(8,128)} fusion(f32[384,384]{1,0:T(8,128)} %get-tuple-element.93, f32[4,384]{1,0:T(4,128)S(1)} %get-tuple-element.79, f32[4,384]{1,0:T(4,128)S(1)} %mul.576, f32[384,384]{1,0:T(8,128)} %get-tuple-element.92, pred[384,384]{1,0:T(8,128)(4,1)S(1)} %copy-done.6, pred[384,384]{1,0:T(8,128)(4,1)S(1)} %copy-done.7, ...), kind=kOutput, calls=%fused_computation.7 | convolution fusion | flops 910098432 | bytes 4632576 | tf_op jit(solution)/shard_map/vmap(vmap())/dot_general | solution.py:57
  86.6 11.2 %while.1 = (s32[]{:T(128)}, f32[4,1,384,384]{3,2,1,0:T(8,128)}, s32[3,2]{0,1:T(2,128)S(1)}, f32[3,4,1,128,128]{4,3,0,2,1:T(8,128)}, s32[]{:T(128)}) while((s32[]{:T(128)}, f32[4,1,384,384]{3,2,1,0:T(8,128)}, s32[3,2]{0,1:T(2,128)S(1)}, f32[3,4,1,128,128]{4,3,0,2,1:T(8,128)}, s32[]{:T(128)}) %tuple.56), condition=%wide.while_cond, body=%wide.while_body.sunk | while | flops 2 | bytes 525421 | solution.py:63
  86.7 0.6 fusion.144
  87.3 3.1 bitcast_dynamic-update-slice_fusion.2
  90.5 0.6 fusion.144
  91.0 3.1 bitcast_dynamic-update-slice_fusion.2
  94.2 0.6 fusion.144
  94.8 3.0 bitcast_dynamic-update-slice_fusion.2
  97.8 118.9 %custom-call.4 = f32[4,1,3,128,128]{3,4,2,1,0:T(8,128)S(1)} custom-call(f32[4,1,3,128,128]{4,3,2,1,0:T(8,128)} %bitcast.622), custom_call_target="InvertDiagBlocksLowerTriangular" | custom-call | tf_op jit(solution)/shard_map/vmap(vmap(jit(_solve_triangular)))/triangular_solve | solution.py:63
  216.7 0.9 fusion.11
  217.6 0.6 fusion.34
  218.3 1.4 fusion.13
  219.7 0.6 convolution_bitcast_fusion.2
  220.3 1.7 fusion.15
  222.0 0.6 convolution_bitcast_fusion
  222.6 0.4 fusion.39
  223.0 0.7 convolution_multiply_fusion.2
  223.7 1.1 convolution_multiply_fusion.1
  224.8 1.0 multiply_reduce_fusion.2
  225.8 0.8 fusion.36
  226.6 2.1 copy.202
  228.7 5.1 %all-to-all-start = ((bf16[128,16,128]{0,2,1:T(8,128)(2,1)}), bf16[128,16,128]{0,2,1:T(8,128)(2,1)S(1)}, u32[]{:S(2)}, u32[]{:S(2)}) async-start(bf16[128,16,128]{0,2,1:T(8,128)(2,1)} %bitcast.33), calls=%async_computation | async-start | bytes 1048576 | tf_op jit(solution)/shard_map/all_to_all | solution.py:154
  233.9 19.0 %all-to-all-done = bf16[128,16,128]{0,2,1:T(8,128)(2,1)S(1)} async-done(((bf16[128,16,128]{0,2,1:T(8,128)(2,1)}), bf16[128,16,128]{0,2,1:T(8,128)(2,1)S(1)}, u32[]{:S(2)}, u32[]{:S(2)}) %all-to-all-start) | async-done | bytes 524320 | tf_op jit(solution)/shard_map/all_to_all | solution.py:154
  252.8 0.3 copy.203
  253.1 20.5 %all-gather.13.cloned.1.call-done = bf16[512,2048]{1,0:T(8,128)(2,1)} async-done(((bf16[512,128]{1,0:T(8,128)(2,1)}), bf16[512,2048]{1,0:T(8,128)(2,1)}) %all-gather.13.cloned.1.call-update) | async-done | bytes 2097168 | tf_op jit(solution)/shard_map/all_gather | solution.py:156
  273.6 2.3 fusion.18
  276.0 0.6 gather_fusion
  276.6 0.9 stack.3
  277.6 15.5 %all-to-all-start.1 = ((bf16[512,1,4,128]{3,2,1,0:T(4,128)(2,1)}), bf16[512,1,4,128]{3,2,1,0:T(4,128)(2,1)S(1)}, u32[]{:S(2)}, u32[]{:S(2)}) async-start(bf16[512,1,4,128]{3,2,1,0:T(4,128)(2,1)} %stack.3), calls=%async_computation.1 | async-start | bytes 1048576 | tf_op jit(solution)/shard_map/all_to_all | solution.py:166
  293.2 0.5 broadcast_multiply_fusion
  293.7 2.1 fusion.17
  295.9 19.9 %all-to-all-done.1 = bf16[512,1,4,128]{3,2,1,0:T(4,128)(2,1)S(1)} async-done(((bf16[512,1,4,128]{3,2,1,0:T(4,128)(2,1)}), bf16[512,1,4,128]{3,2,1,0:T(4,128)(2,1)S(1)}, u32[]{:S(2)}, u32[]{:S(2)}) %all-to-all-start.1) | async-done | bytes 524320 | tf_op jit(solution)/shard_map/all_to_all | solution.py:166
  316.0 0.4 multiply_reduce_fusion
  316.8 0.5 fusion.133
  317.3 15.6 %all-gather.4 = f32[8,3,128]{2,1,0:T(4,128)S(1)} all-gather(f32[1,3,128]{2,1,0:T(4,128)S(1)} %maximum_bitcast_fusion.5), channel_id=2, replica_groups=mesh['batch_0'=8,'batch_1'=4,'head_0'=8,'head_1'=2] {'batch_0'}, dimensions={0}, use_global_device_ids=true | all-gather | bytes 13824 | tf_op jit(solution)/shard_map/all_gather | solution.py:26
  333.0 8.1 %all-gather.5 = f32[4,3,128]{2,1,0:T(4,128)S(1)} all-gather(f32[1,3,128]{2,1,0:T(4,128)S(1)} %maximum_bitcast_fusion.6), channel_id=3, replica_groups=mesh['batch_0'=8,'batch_1'=4,'head_0'=8,'head_1'=2] {'batch_1'}, dimensions={0}, use_global_device_ids=true | all-gather | bytes 7680 | tf_op jit(solution)/shard_map/all_gather | solution.py:26
  341.2 15.6 %all-gather.6 = f32[8,3,128]{2,1,0:T(4,128)S(1)} all-gather(f32[1,3,128]{2,1,0:T(4,128)S(1)} %maximum_bitcast_fusion.7), channel_id=4, replica_groups=mesh['batch_0'=8,'batch_1'=4,'head_0'=8,'head_1'=2] {'head_0'}, dimensions={0}, use_global_device_ids=true | all-gather | bytes 13824 | tf_op jit(solution)/shard_map/all_gather | solution.py:26
  356.8 14.8 %all-gather.7 = f32[2,3,128]{2,1,0:T(4,128)S(1)} all-gather(f32[1,3,128]{2,1,0:T(4,128)S(1)} %maximum_bitcast_fusion.8), channel_id=5, replica_groups=mesh['batch_0'=8,'batch_1'=4,'head_0'=8,'head_1'=2] {'head_1'}, dimensions={0}, use_global_device_ids=true | all-gather | bytes 4608 | tf_op jit(solution)/shard_map/all_gather | solution.py:26
  371.6 0.5 fusion.49
  (104 shorter events, 2.6 us)
Async XLA Ops:
  7.2 309.6 %copy-start = (bf16[32,2048]{1,0:T(8,128)(2,1)S(1)}, bf16[32,2048]{1,0:T(8,128)(2,1)}, u32[]{:S(2)}) copy-start(bf16[32,2048]{1,0:T(8,128)(2,1)} %param.22) | copy-start | bytes 393220
  7.2 54.0 %copy-start.20 = (bf16[2048,4]{0,1:T(4,128)(2,1)S(1)}, bf16[2048,4]{0,1:T(4,128)(2,1)}, u32[]{:S(2)}) copy-start(bf16[2048,4]{0,1:T(4,128)(2,1)} %param.17) | copy-start | bytes 49156
  7.2 54.0 %copy-start.21 = (f32[2048]{0:T(1024)S(1)}, f32[2048]{0:T(1024)}, u32[]{:S(2)}) copy-start(f32[2048]{0:T(1024)} %param.15) | copy-start | bytes 24580
  7.2 51.9 %all-gather.11.cloned.1.call-start = ((), (), s32[]{:S(2)}) async-start(), calls=%async_computation.2 | async-start | bytes 2228224 | tf_op jit(solution)/shard_map/all_gather | solution.py:135
  7.9 265.7 %all-gather.13.cloned.1.call-start = ((), (), s32[]{:S(2)}) async-start(), calls=%async_computation.3 | async-start | bytes 2228224 | tf_op jit(solution)/shard_map/all_gather | solution.py:156
  13.2 50.4 %copy-start.17 = (s32[4]{0:T(128)S(1)}, s32[4]{0:T(128)}, u32[]{:S(2)}) copy-start(s32[4]{0:T(128)} %param.13) | copy-start | bytes 52
  61.2 5.0 %copy-start.1 = (bf16[512,2048]{1,0:T(8,128)(2,1)S(1)}, bf16[512,2048]{1,0:T(8,128)(2,1)}, u32[]{:S(2)}) copy-start(bf16[512,2048]{1,0:T(8,128)(2,1)} %all-gather.11.cloned.1.call-done) | copy-start | bytes 6291460
  63.6 13.1 %copy-start.9 = (f32[4,128,1,4]{1,0,3,2:T(4,128)}, f32[4,128,1,4]{1,0,3,2:T(4,128)S(1)}, u32[]{:S(2)}) copy-start(f32[4,128,1,4]{1,0,3,2:T(4,128)S(1)} %reshape.1819) | copy-start | bytes 24580
  78.6 0.9 slice-start
  78.6 1.1 copy-start.16
  78.9 2.4 copy-start.6
  79.0 2.3 copy-start.7
  80.8 0.5 copy-start.13
  81.3 5.3 %copy-start.10 = (f32[4,384]{1,0:T(4,128)}, f32[4,384]{1,0:T(4,128)S(1)}, u32[]{:S(2)}) copy-start(f32[4,384]{1,0:T(4,128)S(1)} %get-tuple-element.79) | copy-start | bytes 18436
  81.3 5.3 %copy-start.22 = (s32[3]{0:T(128)S(1)}, s32[3]{0:T(128)}, u32[]{:S(2)}) copy-start(s32[3]{0:T(128)} %iota_multiply_fusion) | copy-start | bytes 40
  86.6 130.1 %copy-start.2 = (f32[4,1,128,128]{3,2,1,0:T(8,128)S(1)}, f32[4,1,128,128]{3,2,1,0:T(8,128)}, u32[]{:S(2)}) copy-start(f32[4,1,128,128]{3,2,1,0:T(8,128)} %param.14) | copy-start | bytes 786436
  218.2 4.7 %copy-start.4 = (f32[4,128,1,1,128]{4,3,1,0,2:T(1,128)S(1)}, f32[4,128,1,1,128]{4,3,1,0,2:T(1,128)}, u32[]{:S(2)}) copy-start(f32[4,128,1,1,128]{4,3,1,0,2:T(1,128)} %slice.495) | copy-start | bytes 786436
  219.7 4.0 %copy-start.8 = (pred[128,384]{1,0:T(8,128)(4,1)S(1)}, pred[128,384]{1,0:T(8,128)(4,1)}, u32[]{:S(2)}) copy-start(pred[128,384]{1,0:T(8,128)(4,1)} %iota_compare_fusion.4) | copy-start | bytes 147460
  219.7 4.0 %copy-start.11 = (f32[4,384]{1,0:T(4,128)S(1)}, f32[4,384]{1,0:T(4,128)}, u32[]{:S(2)}) copy-start(f32[4,384]{1,0:T(4,128)} %copy-done.10) | copy-start | bytes 18436
  223.7 2.1 copy-start.15
  224.8 9.0 %copy-start.18 = (s32[4]{0:T(128)S(1)}, s32[4]{0:T(128)}, u32[]{:S(2)}) copy-start(s32[4]{0:T(128)} %param.13) | copy-start | bytes 52
  225.8 47.9 %copy-start.3 = (bf16[512,128]{1,0:T(8,128)(2,1)S(1)}, bf16[512,128]{1,0:T(8,128)(2,1)}, u32[]{:S(2)}) copy-start(bf16[512,128]{1,0:T(8,128)(2,1)} %param.12) | copy-start | bytes 393220
  228.7 24.2 %all-to-all-start = ((bf16[128,16,128]{0,2,1:T(8,128)(2,1)}), bf16[128,16,128]{0,2,1:T(8,128)(2,1)S(1)}, u32[]{:S(2)}, u32[]{:S(2)}) async-start(bf16[128,16,128]{0,2,1:T(8,128)(2,1)} %bitcast.33), calls=%async_computation | async-start | bytes 1048576 | tf_op jit(solution)/shard_map/all_to_all | solution.py:154
  253.1 39.9 %copy-start.14 = (f32[4]{0:T(128)S(1)}, f32[4]{0:T(128)}, u32[]{:S(2)}) copy-start(f32[4]{0:T(128)} %copy-done.13) | copy-start | bytes 52
  275.9 19.9 %copy-start.5 = (bf16[512,128]{1,0:T(8,128)(2,1)}, bf16[512,128]{1,0:T(8,128)(2,1)S(1)}, u32[]{:S(2)}) copy-start(bf16[512,128]{1,0:T(8,128)(2,1)S(1)} %fusion.18) | copy-start | bytes 393220
  277.6 38.2 %all-to-all-start.1 = ((bf16[512,1,4,128]{3,2,1,0:T(4,128)(2,1)}), bf16[512,1,4,128]{3,2,1,0:T(4,128)(2,1)S(1)}, u32[]{:S(2)}, u32[]{:S(2)}) async-start(bf16[512,1,4,128]{3,2,1,0:T(4,128)(2,1)} %stack.3), calls=%async_computation.1 | async-start | bytes 1048576 | tf_op jit(solution)/shard_map/all_to_all | solution.py:166
  295.9 20.9 %copy-start.12 = (f32[2048]{0:T(1024)S(1)}, f32[2048]{0:T(1024)}, u32[]{:S(2)}) copy-start(f32[2048]{0:T(1024)} %param.21) | copy-start | bytes 24580
  315.8 1.4 copy-start.19
Sparse Core Ops, SparseCore 0:
  10.1 48.9 all-gather.10
  226.7 46.8 all-gather.12
